TPU v7x, 16 devices: a whole 2x2x2 slice. The times are simulated.
16 devices in a mesh: fsdp: 16 (over z, y, x, core).
Axes of the slice: x: 2, y: 2, z: 2, core: 2. Of those that a mesh axis runs over, the one named last changes fastest.
Arguments:
- left_mat: bfloat16 [98304, 1536], P('fsdp')
- right_mat: bfloat16 [1536, 1536], P('fsdp')
Outputs:
- output: bfloat16 [98304, 1536], P('fsdp')
All inputs are finite; a program needn't handle non-finite values.
Results may differ from a plain program's by a relative error of at most 0.001.
Values are sent between devices in bfloat16 or wider.
A program may use at most 1 GiB of HBM per device.

v0:
```python
import jax
import jax.numpy as jnp
from jax import lax
from jax.sharding import PartitionSpec as P


def solution(mesh):
    spec_rows = P("fsdp", None)

    def local_fn(left_blk, right_blk):
        full_right = lax.all_gather(right_blk, "fsdp", axis=0, tiled=True)
        return jnp.dot(left_blk, full_right, preferred_element_type=jnp.float32).astype(jnp.bfloat16)

    return jax.shard_map(local_fn, mesh=mesh, in_specs=(spec_rows, spec_rows), out_specs=spec_rows, check_vma=False)
```

profile of v0, /device:TPU:0, one launch (start us, length us, event | category | flops | bytes accessed | tf_op | source)
XLA Modules:
  0.0 92.0 jit_solution(14257481831629898483)
XLA Ops:
  6.5 0.0 all-gather.2.cloned.1.call-start
  6.5 0.7 all-gather.2.cloned.1.call-update
  7.3 41.8 %all-gather.2.cloned.1.call-done = bf16[1536,1536]{1,0:T(8,128)(2,1)} async-done(((bf16[96,1536]{1,0:T(8,128)(2,1)}), bf16[1536,1536]{1,0:T(8,128)(2,1)}) %all-gather.2.cloned.1.call-update) | async-done | bytes 4718608 | tf_op jit(solution)/shard_map/all_gather | solution.py:11
  49.1 36.1 %convolution_convert_fusion = bf16[6144,1536]{1,0:T(8,128)(2,1)} fusion(bf16[6144,1536]{1,0:T(8,128)(2,1)} %param.2, bf16[1536,1536]{1,0:T(8,128)(2,1)} %all-gather.2.cloned.1.call-done), kind=kOutput, calls=%fused_computation | convolution fusion | flops 29000466432 | bytes 42467328 | tf_op jit(solution)/shard_map/dot_general | solution.py:12
Async XLA Ops:
  6.5 42.5 %all-gather.2.cloned.1.call-start = ((), (), s32[]{:S(2)}) async-start(), calls=%async_computation | async-start | bytes 5013504 | tf_op jit(solution)/shard_map/all_gather | solution.py:11
Sparse Core Ops, SparseCore 0:
  9.6 39.4 all-gather.1
where the time goes:
time: 92.1 us; the launch traced here: 92 us
  waiting for transfers between devices  42.5 us (46%)
  matrix products  36.1 us (39%)
  between operations  13.4 us (15%)
    all_gather x1, waiting for transfers between devices, local_fn(): full_right = lax.all_gather(right_blk, 'fsdp', axis=0, tiled=True)  41.8 us
    dot_general x1, matrix products, local_fn(): jnp.dot(left_blk, full_right, preferred_element_type=jnp.float32)  36.1 us
  transfers between devices with their start and end apart: 1, of which 1 were waited for; matrix products, arithmetic and copies ran while one was open for 0% of the time, Pallas kernels for 0%

commit v1 on v0

v1 whole, which is shorter than its diff:
```python
import jax
import jax.numpy as jnp
from jax import lax
from jax.experimental import pallas as pl
from jax.experimental.pallas import tpu as pltpu
from jax.sharding import PartitionSpec as P

MESH = pl.DeviceIdType.MESH
BF16, F32 = jnp.bfloat16, jnp.float32

W = 256
KT = 256
TM = 1024
HALF = TM // 2
SLOTS = 4
LIMIT = 20 * 2**20
FIRST = 5
PEERS = (2, 4, 8, 6, 10, 12, 14)


class Steps:
    def __init__(self, accs, a, b, flush):
        self.accs = ((accs[0], accs[1]), (accs[2], accs[3]))
        self.a, self.b, self.flush = a, b, flush
        self.n, self.last, self.staged = 0, None, False

    def push(self, unit, block, k, reg):
        pltpu.matmul_push_rhs(self.b[block, pl.ds(k * KT, KT), :], staging_register=reg, mxu_index=unit)

    def step(self, block, tile, passes, following=None):
        side = self.n % 2
        if not self.staged:
            for unit in range(2):
                self.push(unit, block, passes[0], 0)
        for p, k in enumerate(passes):
            nxt = (block, passes[p + 1]) if p + 1 < len(passes) else following
            if nxt is not None:
                reg = (p + 1) % 2 if p + 1 < len(passes) else 0
                for unit in range(2):
                    self.push(unit, *nxt, reg)
            for unit in range(2):
                rows = pl.ds(tile * TM + unit * HALF, HALF)
                pltpu.matmul_acc_lhs(
                    self.accs[unit][side], self.a[rows, pl.ds(k * KT, KT)], load_staged_rhs=p % 2
                )
        self.staged = following is not None
        self.drain()
        self.last = (block, tile, side)
        self.n += 1

    def drain(self):
        if self.last is not None:
            block, tile, side = self.last
            self.flush(block, tile, [self.accs[unit][side] for unit in range(2)])
            self.last = None


def first_kernel(blocks, a_hbm, b_hbm, a, b, c, own, load_sem, a_sem, send_sem, recv_sem, pair_sem):
    tiles, groups = a.shape[0] // TM, 4
    depth = own.shape[0]
    span = a.shape[1] // groups
    me = lax.axis_index("fsdp")
    lane, plane = lax.rem(me, 4), me // 4

    load = pltpu.make_async_copy(b_hbm, own, load_sem)
    load.start()
    barrier = pltpu.get_barrier_semaphore()
    for mask in (1, *PEERS):
        pl.semaphore_signal(barrier, inc=1, device_id=(me ^ mask,), device_id_type=MESH)

    def a_copy(tile, group):
        rows = pl.ds(tile * TM, TM)
        there = pl.ds(pl.multiple_of((plane ^ group) * span, 128), span)
        return pltpu.make_async_copy(
            a_hbm.at[rows, there], a.at[rows, pl.ds(group * span, span)], a_sem.at[tile, group]
        )

    for group in range(groups):
        for tile in range(tiles):
            a_copy(tile, group).start()

    pl.semaphore_wait(barrier, 1 + len(PEERS))
    load.wait()

    def rows_of(mask, at):
        return pl.ds(pl.multiple_of((mask // 4) * span + (lax.rem(at, 4) ^ (mask % 4)) * depth, 32), depth)

    def columns(block):
        return pl.ds(pl.multiple_of(block * W, W), W)

    def send(block, mask):
        pltpu.make_async_remote_copy(
            src_ref=own.at[:, columns(block)],
            dst_ref=b.at[block, rows_of(mask, me ^ mask), :],
            send_sem=send_sem.at[block],
            recv_sem=(pair_sem if mask == 1 else recv_sem).at[block],
            device_id=(me ^ mask,),
            device_id_type=MESH,
        ).start()

    def hand_on(block, mask):
        pltpu.make_async_remote_copy(
            src_ref=b.at[block, rows_of(mask, me), :],
            dst_ref=b.at[block, rows_of(mask, me), :],
            send_sem=send_sem.at[block],
            recv_sem=pair_sem.at[block],
            device_id=(me ^ 1,),
            device_id_type=MESH,
        ).start()

    def wait_rows(sem, block, count):
        part = b.at[block, pl.ds(0, count * depth), :]
        pltpu.make_async_copy(part, part, sem.at[block]).wait()

    def send_block(block, carry):
        for mask in (*PEERS, 1):
            send(block, mask)
        b[block, rows_of(0, me), :] = own[:, columns(block)]
        return carry

    lax.fori_loop(0, blocks, send_block, 0)

    def arrived(block):
        wait_rows(recv_sem, block, len(PEERS))
        for mask in PEERS:
            hand_on(block, mask)

    def complete(block):
        wait_rows(pair_sem, block, 1 + len(PEERS))

    def multiply(block, part):
        quarter = a.shape[0] // 4
        for piece in (2 * part, 2 * part + 1):
            rows = pl.ds(piece * quarter, quarter)
            c[block, rows, :] = jnp.dot(a[rows, :], b[block], preferred_element_type=F32).astype(BF16)

    arrived(0)
    for tile in range(tiles):
        for group in range(groups):
            a_copy(tile, group).wait()

    def one_block(block, carry):
        complete(block)
        multiply(block, 0)
        arrived(block + 1)
        multiply(block, 1)
        return carry

    lax.fori_loop(0, FIRST, one_block, 0)
    for block in range(FIRST, blocks):
        if block > FIRST:
            arrived(block)
        complete(block)
    for block in range(blocks):
        wait_rows(send_sem, block, 1 + 2 * len(PEERS))


def second_kernel(blocks, a, b, c, out, stage, out_sem, c_sem):
    tiles = a.shape[0] // TM

    def done_copy(block):
        return pltpu.make_async_copy(c.at[block], out.at[:, pl.ds(block * W, W)], c_sem.at[block])

    for block in range(FIRST):
        done_copy(block).start()

    used = []

    def out_copy(block, tile, slot):
        return pltpu.make_async_copy(
            stage.at[slot], out.at[pl.ds(tile * TM, TM), pl.ds(block * W, W)], out_sem.at[slot]
        )

    def flush(block, tile, accs):
        n = len(used)
        slot = n % SLOTS
        for unit in range(2):
            stage[slot, pl.ds(unit * HALF, HALF), :] = pltpu.matmul_pop(accs[unit]).astype(BF16)
        out_copy(block, tile, slot).start()
        used.append((block, tile, slot))

    def body(*accs):
        steps = Steps(accs, a, b, flush)
        order = [(block, tile) for block in range(FIRST, blocks) for tile in range(tiles)]
        for at, (block, tile) in enumerate(order):
            if at > SLOTS:
                out_copy(*used[at - 1 - SLOTS]).wait()
            steps.step(block, tile, range(6), (order[at + 1][0], 0) if at + 1 < len(order) else None)
        if len(order) > SLOTS:
            out_copy(*used[len(order) - 1 - SLOTS]).wait()
        steps.drain()
        for copy in used[max(0, len(order) - SLOTS) :]:
            out_copy(*copy).wait()

    pl.run_scoped(body, *[pltpu.ACC(unit)((HALF, W), F32) for unit in (0, 0, 1, 1)])
    for block in range(FIRST):
        done_copy(block).wait()


def solution(mesh):
    def step(a, b):
        (rows, depth), (own, columns) = a.shape, b.shape
        blocks, tiles = columns // W, rows // TM
        dma = pltpu.SemaphoreType.DMA
        vmem, hbm = pl.BlockSpec(memory_space=pltpu.VMEM), pl.BlockSpec(memory_space=pltpu.HBM)
        a, b, c = pl.pallas_call(
            lambda *refs: first_kernel(blocks, *refs),
            name="first",
            out_shape=(
                pltpu.VMEM((rows, depth), BF16),
                pltpu.VMEM((blocks, depth, W), BF16),
                pltpu.VMEM((FIRST, rows, W), BF16),
            ),
            in_specs=[hbm, hbm],
            out_specs=(vmem, vmem, vmem),
            scratch_shapes=[
                pltpu.VMEM((own, columns), BF16),
                dma,
                dma((tiles, 4)),
                dma((blocks,)),
                dma((blocks,)),
                dma((blocks,)),
            ],
            compiler_params=pltpu.CompilerParams(
                vmem_limit_bytes=LIMIT, collective_id=0, has_side_effects=True
            ),
        )(a, b)
        a, b, c = (pltpu.with_memory_space_constraint(x, pltpu.VMEM) for x in (a, b, c))
        return pl.pallas_call(
            lambda *refs: second_kernel(blocks, *refs),
            name="second",
            out_shape=jax.ShapeDtypeStruct((rows, columns), BF16),
            in_specs=[vmem, vmem, vmem],
            out_specs=hbm,
            scratch_shapes=[pltpu.VMEM((SLOTS, TM, W), BF16), dma((SLOTS,)), dma((FIRST,))],
            compiler_params=pltpu.CompilerParams(vmem_limit_bytes=LIMIT),
        )(a, b, c)

    spec = P("fsdp", None)
    return jax.shard_map(step, mesh=mesh, in_specs=(spec, spec), out_specs=spec, check_vma=False)
```

time: 92.1 us -> 48.7 us (0.53)
  Pallas kernels: 0 us -> 48.6 us
  waiting for transfers between devices: 42.5 us -> 0 us
  matrix products: 36.1 us -> 0 us
  between operations: 13.4 us -> 0.01 us
    pallas_call x0 -> x2, Pallas kernels: none -> 48.6 us  [the longest x1 41 us: step(): pl.pallas_call(lambda *refs: first_kernel(blocks, *refs), name='first', o...]
    all_gather x1 -> x0, waiting for transfers between devices: 41.8 us -> none  [local_fn(): full_right = lax.all_gather(right_blk, 'fsdp', axis=0, tiled=True)]
    dot_general x1 -> x0, matrix products: 36.1 us -> none  [local_fn(): jnp.dot(left_blk, full_right, preferred_element_type=jnp.float32)]
  transfers between devices with their start and end apart: 1 -> 0, of which waited for: 1 -> 0; matrix products, arithmetic and copies ran while one was open for 0% -> 0% of each run, Pallas kernels for 0% -> 0%
where the time goes in v1:
time: 48.7 us; the launch traced here: 48.6 us
  Pallas kernels  48.6 us (100%)
    pallas_call x1, Pallas kernels, step(): pl.pallas_call(lambda *refs: first_kernel(blocks, *refs), name='first', o...  41 us
    pallas_call x1, Pallas kernels, step(): pl.pallas_call(lambda *refs: second_kernel(blocks, *refs), name='second',...  7.55 us

profile of v1, /device:TPU:0, one launch (start us, length us, event | category | flops | bytes accessed | tf_op | source)
XLA Modules:
  0.0 48.6 jit_solution(3091756550379896017)
XLA Ops:
  0.0 41.0 %first.1 = (bf16[6144,1536]{1,0:T(8,128)(2,1)S(1)}, bf16[6,1536,256]{2,1,0:T(8,128)(2,1)S(1)}, bf16[5,6144,256]{2,1,0:T(8,128)(2,1)S(1)}) custom-call(bf16[6144,1536]{1,0:T(8,128)(2,1)} %refs_0_.1, bf16[96,1536]{1,0:T(8,128)(2,1)} %refs_1_.1), custom_call_target="tpu_custom_call" | custom-call | tf_op jit(solution)/shard_map/first/pallas_call | solution.py:206
  41.1 7.6 %second.1 = bf16[6144,1536]{1,0:T(8,128)(2,1)} custom-call(bf16[6144,1536]{1,0:T(8,128)(2,1)S(1)} %get-tuple-element.8.refs_0_, bf16[6,1536,256]{2,1,0:T(8,128)(2,1)S(1)} %get-tuple-element.9.refs_1_, bf16[5,6144,256]{2,1,0:T(8,128)(2,1)S(1)} %get-tuple-element.10.refs_2_), custom_call_target="tpu_custom_call" | custom-call | tf_op jit(solution)/shard_map/second/pallas_call | solution.py:229

commit v2 on v1

--- a/solution.py
+++ b/solution.py
@@ -1,3 +1,5 @@
+import functools
+
 import jax
 import jax.numpy as jnp
 from jax import lax
@@ -12,10 +14,12 @@
 KT = 256
 TM = 1024
 HALF = TM // 2
-SLOTS = 4
+SLOTS = 8
 LIMIT = 20 * 2**20
-FIRST = 5
-PEERS = (2, 4, 8, 6, 10, 12, 14)
+WHOLE = 4
+PART = 4
+NEAR, FAR = (2, 4, 6), (8, 10, 12, 14)
+PEERS = NEAR + FAR
 
 
 class Steps:
@@ -55,12 +59,12 @@
             self.last = None
 
 
-def first_kernel(blocks, a_hbm, b_hbm, a, b, c, own, load_sem, a_sem, send_sem, recv_sem, pair_sem):
+def first_kernel(blocks, a_hbm, b_hbm, a, b, c, own, partial, load_sem, a_sem, send_sem, recv_sem, pair_sem):
     tiles, groups = a.shape[0] // TM, 4
     depth = own.shape[0]
     span = a.shape[1] // groups
     me = lax.axis_index("fsdp")
-    lane, plane = lax.rem(me, 4), me // 4
+    plane = me // 4
 
     load = pltpu.make_async_copy(b_hbm, own, load_sem)
     load.start()
@@ -83,85 +87,126 @@
     load.wait()
 
     def rows_of(mask, at):
-        return pl.ds(pl.multiple_of((mask // 4) * span + (lax.rem(at, 4) ^ (mask % 4)) * depth, 32), depth)
+        return pl.ds(pl.multiple_of((mask // 4) * span + (at % 4 ^ mask % 4) * depth, 32), depth)
 
     def columns(block):
         return pl.ds(pl.multiple_of(block * W, W), W)
 
-    def send(block, mask):
+    first = me % 8 - me % 2
+
+    def send(block, mask, half):
         pltpu.make_async_remote_copy(
             src_ref=own.at[:, columns(block)],
             dst_ref=b.at[block, rows_of(mask, me ^ mask), :],
             send_sem=send_sem.at[block],
-            recv_sem=(pair_sem if mask == 1 else recv_sem).at[block],
+            recv_sem=(pair_sem if isinstance(mask, int) else recv_sem).at[block, half],
             device_id=(me ^ mask,),
             device_id_type=MESH,
         ).start()
 
-    def hand_on(block, mask):
-        pltpu.make_async_remote_copy(
-            src_ref=b.at[block, rows_of(mask, me), :],
-            dst_ref=b.at[block, rows_of(mask, me), :],
-            send_sem=send_sem.at[block],
-            recv_sem=pair_sem.at[block],
-            device_id=(me ^ 1,),
-            device_id_type=MESH,
-        ).start()
-
     def wait_rows(sem, block, count):
         part = b.at[block, pl.ds(0, count * depth), :]
-        pltpu.make_async_copy(part, part, sem.at[block]).wait()
+        pltpu.make_async_copy(part, part, sem).wait()
 
     def send_block(block, carry):
-        for mask in (*PEERS, 1):
-            send(block, mask)
+        for turn in (0, 2, 4, 6):
+            mask = first ^ turn
+            pl.when(mask != 0)(functools.partial(send, block, mask, 0))
+        send(block, 1, 0)
+        for turn in (0, 2, 4, 6):
+            send(block, 8 + (first ^ turn), 1)
         b[block, rows_of(0, me), :] = own[:, columns(block)]
         return carry
 
     lax.fori_loop(0, blocks, send_block, 0)
 
-    def arrived(block):
-        wait_rows(recv_sem, block, len(PEERS))
-        for mask in PEERS:
-            hand_on(block, mask)
-
-    def complete(block):
-        wait_rows(pair_sem, block, 1 + len(PEERS))
-
-    def multiply(block, part):
-        quarter = a.shape[0] // 4
-        for piece in (2 * part, 2 * part + 1):
-            rows = pl.ds(piece * quarter, quarter)
-            c[block, rows, :] = jnp.dot(a[rows, :], b[block], preferred_element_type=F32).astype(BF16)
-
-    arrived(0)
+    def arrived(block, half):
+        masks = (NEAR, FAR)[half]
+        wait_rows(recv_sem.at[block, half], block, len(masks))
+        for mask in masks:
+            pltpu.make_async_remote_copy(
+                src_ref=b.at[block, rows_of(mask, me), :],
+                dst_ref=b.at[block, rows_of(mask, me), :],
+                send_sem=send_sem.at[block],
+                recv_sem=pair_sem.at[block, half],
+                device_id=(me ^ 1,),
+                device_id_type=MESH,
+            ).start()
+
+    def complete(block, half):
+        wait_rows(pair_sem.at[block, half], block, 4)
+
+    middle = 2 * span
+
+    def dots(first, count, each):
+        for piece in range(2):
+            each(pl.ds(first + piece * (count // 2), count // 2))
+
+    def near(block, first, count):
+        def each(rows):
+            partial[rows, :] = jnp.dot(a[rows, :middle], b[block, :middle, :], preferred_element_type=F32)
+
+        dots(first, count, each)
+
+    def far(block, first, count):
+        def each(rows):
+            product = jnp.dot(a[rows, middle:], b[block, middle:, :], preferred_element_type=F32)
+            c[block, rows, :] = (partial[rows, :] + product).astype(BF16)
+
+        dots(first, count, each)
+
+    total = a.shape[0]
+    part = total // 2
+
+    arrived(0, 0)
     for tile in range(tiles):
         for group in range(groups):
             a_copy(tile, group).wait()
 
+    complete(0, 0)
+    near(0, 0, part)
+    arrived(0, 1)
+    near(0, part, part)
+    complete(0, 1)
+    far(0, 0, part)
+    arrived(1, 0)
+    far(0, part, part)
+
     def one_block(block, carry):
-        complete(block)
-        multiply(block, 0)
-        arrived(block + 1)
-        multiply(block, 1)
+        complete(block, 0)
+        arrived(block, 1)
+        near(block, 0, total)
+        complete(block, 1)
+        arrived(block + 1, 0)
+        far(block, 0, total)
         return carry
 
-    lax.fori_loop(0, FIRST, one_block, 0)
-    for block in range(FIRST, blocks):
-        if block > FIRST:
-            arrived(block)
-        complete(block)
+    lax.fori_loop(1, WHOLE, one_block, 0)
+    rows = PART * TM
+    complete(WHOLE, 0)
+    arrived(WHOLE, 1)
+    near(WHOLE, 0, rows)
+    complete(WHOLE, 1)
+    arrived(WHOLE + 1, 0)
+    far(WHOLE, 0, rows // 2)
+    arrived(WHOLE + 1, 1)
+    far(WHOLE, rows // 2, rows // 2)
+    complete(WHOLE + 1, 0)
+    complete(WHOLE + 1, 1)
     for block in range(blocks):
-        wait_rows(send_sem, block, 1 + 2 * len(PEERS))
+        wait_rows(send_sem.at[block], block, 1 + 2 * len(PEERS))
 
 
 def second_kernel(blocks, a, b, c, out, stage, out_sem, c_sem):
     tiles = a.shape[0] // TM
 
     def done_copy(block):
-        return pltpu.make_async_copy(c.at[block], out.at[:, pl.ds(block * W, W)], c_sem.at[block])
-
-    for block in range(FIRST):
+        rows = pl.ds(0, a.shape[0] if block < WHOLE else PART * TM)
+        return pltpu.make_async_copy(
+            c.at[block, rows, :], out.at[rows, pl.ds(block * W, W)], c_sem.at[block]
+        )
+
+    for block in range(WHOLE + 1):
         done_copy(block).start()
 
     used = []
@@ -181,7 +226,8 @@
 
     def body(*accs):
         steps = Steps(accs, a, b, flush)
-        order = [(block, tile) for block in range(FIRST, blocks) for tile in range(tiles)]
+        order = [(WHOLE, tile) for tile in range(PART, tiles)]
+        order += [(block, tile) for block in range(WHOLE + 1, blocks) for tile in range(tiles)]
         for at, (block, tile) in enumerate(order):
             if at > SLOTS:
                 out_copy(*used[at - 1 - SLOTS]).wait()
@@ -193,7 +239,7 @@
             out_copy(*copy).wait()
 
     pl.run_scoped(body, *[pltpu.ACC(unit)((HALF, W), F32) for unit in (0, 0, 1, 1)])
-    for block in range(FIRST):
+    for block in range(WHOLE + 1):
         done_copy(block).wait()
 
 
@@ -209,17 +255,18 @@
             out_shape=(
                 pltpu.VMEM((rows, depth), BF16),
                 pltpu.VMEM((blocks, depth, W), BF16),
-                pltpu.VMEM((FIRST, rows, W), BF16),
+                pltpu.VMEM((WHOLE + 1, rows, W), BF16),
             ),
             in_specs=[hbm, hbm],
             out_specs=(vmem, vmem, vmem),
             scratch_shapes=[
                 pltpu.VMEM((own, columns), BF16),
+                pltpu.VMEM((rows, W), F32),
                 dma,
                 dma((tiles, 4)),
                 dma((blocks,)),
-                dma((blocks,)),
-                dma((blocks,)),
+                dma((blocks, 2)),
+                dma((blocks, 2)),
             ],
             compiler_params=pltpu.CompilerParams(
                 vmem_limit_bytes=LIMIT, collective_id=0, has_side_effects=True
@@ -232,7 +279,7 @@
             out_shape=jax.ShapeDtypeStruct((rows, columns), BF16),
             in_specs=[vmem, vmem, vmem],
             out_specs=hbm,
-            scratch_shapes=[pltpu.VMEM((SLOTS, TM, W), BF16), dma((SLOTS,)), dma((FIRST,))],
+            scratch_shapes=[pltpu.VMEM((SLOTS, TM, W), BF16), dma((SLOTS,)), dma((WHOLE + 1,))],
             compiler_params=pltpu.CompilerParams(vmem_limit_bytes=LIMIT),
         )(a, b, c)
 

time: 48.7 us -> 44.4 us (0.912)
  Pallas kernels: 48.6 us -> 44.1 us
    pallas_call x1, Pallas kernels: 41 us -> 36.5 us  [step(): pl.pallas_call(lambda *refs: first_kernel(blocks, *refs), name='first', o...]
where the time goes in v2:
time: 44.4 us; the launch traced here: 44.3 us
  Pallas kernels  44.1 us (99%)
    pallas_call x1, Pallas kernels, step(): pl.pallas_call(lambda *refs: first_kernel(blocks, *refs), name='first', o...  36.5 us
    pallas_call x1, Pallas kernels, step(): pl.pallas_call(lambda *refs: second_kernel(blocks, *refs), name='second',...  7.58 us

profile of v2, /device:TPU:0, one launch (start us, length us, event | category | flops | bytes accessed | tf_op | source)
XLA Modules:
  0.0 44.3 jit_solution(14433954511193767266)
XLA Ops:
  0.0 36.5 %first.1 = (bf16[6144,1536]{1,0:T(8,128)(2,1)S(1)}, bf16[6,1536,256]{2,1,0:T(8,128)(2,1)S(1)}, bf16[5,6144,256]{2,1,0:T(8,128)(2,1)S(1)}) custom-call(bf16[6144,1536]{1,0:T(8,128)(2,1)} %refs_0_.1, bf16[96,1536]{1,0:T(8,128)(2,1)} %refs_1_.1), custom_call_target="tpu_custom_call" | custom-call | tf_op jit(solution)/shard_map/first/pallas_call | solution.py:252
  36.5 7.6 %second.1 = bf16[6144,1536]{1,0:T(8,128)(2,1)} custom-call(bf16[6144,1536]{1,0:T(8,128)(2,1)S(1)} %get-tuple-element.8.refs_0_, bf16[6,1536,256]{2,1,0:T(8,128)(2,1)S(1)} %get-tuple-element.9.refs_1_, bf16[5,6144,256]{2,1,0:T(8,128)(2,1)S(1)} %get-tuple-element.10.refs_2_), custom_call_target="tpu_custom_call" | custom-call | tf_op jit(solution)/shard_map/second/pallas_call | solution.py:276

commit v3 on v2

v3 whole, which is shorter than its diff:
```python
import functools

import jax
import jax.numpy as jnp
from jax import lax
from jax.experimental import pallas as pl
from jax.experimental.pallas import tpu as pltpu
from jax.sharding import PartitionSpec as P

MESH = pl.DeviceIdType.MESH
BF16, F32 = jnp.bfloat16, jnp.float32

W = 256
KT = 256
TM = 1024
STEP = 512
HALF = STEP // 2
LIMIT = 20 * 2**20
WHOLE = 4
EARLY = 4
PART = 4
NEAR, FAR = (2, 4, 6), (14, 10, 12, 8)
PEERS = NEAR + FAR
PAIR = 1
GREETED = (1, 2, 4, 6, 8)


class Steps:
    def __init__(self, accs, a, b, flush):
        self.accs = ((accs[0], accs[1]), (accs[2], accs[3]))
        self.a, self.b, self.flush = a, b, flush
        self.n, self.last, self.staged = 0, None, False

    def push(self, unit, block, k, reg):
        pltpu.matmul_push_rhs(self.b[block, pl.ds(k * KT, KT), :], staging_register=reg, mxu_index=unit)

    def step(self, block, tile, passes, following=None):
        side = self.n % 2
        if not self.staged:
            for unit in range(2):
                self.push(unit, block, passes[0], 0)
        for p, k in enumerate(passes):
            nxt = (block, passes[p + 1]) if p + 1 < len(passes) else following
            if nxt is not None:
                reg = (p + 1) % 2 if p + 1 < len(passes) else 0
                for unit in range(2):
                    self.push(unit, *nxt, reg)
            for unit in range(2):
                rows = pl.ds(tile * STEP + unit * HALF, HALF)
                pltpu.matmul_acc_lhs(
                    self.accs[unit][side], self.a[rows, pl.ds(k * KT, KT)], load_staged_rhs=p % 2
                )
        self.staged = following is not None
        self.drain()
        self.last = (block, tile, side)
        self.n += 1

    def drain(self):
        if self.last is not None:
            block, tile, side = self.last
            self.flush(block, tile, [self.accs[unit][side] for unit in range(2)])
            self.last = None


def first_kernel(blocks, a_hbm, b_hbm, a, b, c, partial, load_sem, a_sem, send_sem, recv_sem, pair_sem, ready):
    tiles, groups = a.shape[0] // TM, 4
    depth = b_hbm.shape[0]
    span = a.shape[1] // groups
    me = lax.axis_index("fsdp")
    plane = me // 4

    def rows_of(mask, at):
        return pl.ds(pl.multiple_of((mask // 4) * span + (at % 4 ^ mask % 4) * depth, 32), depth)

    def load(block):
        there = pl.ds(pl.multiple_of(block * W, W), W)
        return pltpu.make_async_copy(b_hbm.at[:, there], b.at[block, rows_of(0, me), :], load_sem.at[block])

    for block in range(blocks):
        load(block).start()
    barrier = pltpu.get_barrier_semaphore()
    for mask in GREETED:
        pl.semaphore_signal(barrier, inc=1, device_id=(me ^ mask,), device_id_type=MESH)

    def a_copy(tile, group):
        rows = pl.ds(tile * TM, TM)
        there = pl.ds(pl.multiple_of((plane ^ group) * span, 128), span)
        return pltpu.make_async_copy(
            a_hbm.at[rows, there], a.at[rows, pl.ds(group * span, span)], a_sem.at[tile, group]
        )

    for group in range(groups):
        for tile in range(tiles):
            a_copy(tile, group).start()

    pl.semaphore_wait(barrier, len(GREETED))
    pl.semaphore_signal(ready, inc=1, device_id=(me ^ 8,), device_id_type=MESH)
    load(0).wait()

    first = me % 8 - me % 2

    def send(block, mask, half):
        pltpu.make_async_remote_copy(
            src_ref=b.at[block, rows_of(0, me), :],
            dst_ref=b.at[block, rows_of(mask, me ^ mask), :],
            send_sem=send_sem.at[block],
            recv_sem=recv_sem.at[block, half],
            device_id=(me ^ mask,),
            device_id_type=MESH,
        ).start()

    chips = b.reshape(blocks, 8, 2 * depth, W)

    def wait_rows(sem, block, count):
        part = b.at[block, pl.ds(0, count * depth), :]
        pltpu.make_async_copy(part, part, sem).wait()

    def send_near(block):
        for turn in (0, 2, 4, 6):
            mask = first ^ turn
            pl.when(mask != 0)(functools.partial(send, block, mask, 0))

    def send_far(block):
        for mask in (14, 10, 12, 8):
            send(block, mask, 1)

    def send_block(block, carry):
        load(block).wait()
        send_near(block)
        send_far(block)
        return carry

    send_near(0)
    pl.semaphore_wait(ready, 1)
    send_far(0)
    lax.fori_loop(1, blocks, send_block, 0)

    def arrived(block, half):
        wait_rows(recv_sem.at[block, half], block, len((NEAR, FAR)[half]))
        mine = chips.at[block, pl.ds(4 * half, 4), pl.ds(pl.multiple_of(me % 2 * depth, 32), depth), :]
        pltpu.make_async_remote_copy(
            src_ref=mine,
            dst_ref=mine,
            send_sem=send_sem.at[block],
            recv_sem=pair_sem.at[block, half],
            device_id=(me ^ PAIR,),
            device_id_type=MESH,
        ).start()

    def complete(block, half):
        wait_rows(pair_sem.at[block, half], block, 4)

    middle = 2 * span

    def dots(first, count, each):
        for piece in range(2):
            each(pl.ds(first + piece * (count // 2), count // 2))

    def near(block, first, count):
        def each(rows):
            partial[rows, :] = jnp.dot(a[rows, :middle], b[block, :middle, :], preferred_element_type=F32)

        dots(first, count, each)

    def full(block, first, count):
        def each(rows):
            c[block, rows, :] = jnp.dot(a[rows, :], b[block], preferred_element_type=F32).astype(BF16)

        dots(first, count, each)

    def far(block, first, count):
        def each(rows):
            product = jnp.dot(a[rows, middle:], b[block, middle:, :], preferred_element_type=F32)
            c[block, rows, :] = (partial[rows, :] + product).astype(BF16)

        dots(first, count, each)

    total = a.shape[0]
    part = total // 2

    arrived(0, 0)
    for tile in range(tiles):
        for group in range(groups):
            a_copy(tile, group).wait()

    early = EARLY * TM
    complete(0, 0)
    near(0, 0, early)
    arrived(0, 1)
    near(0, early, total - early)
    complete(0, 1)
    far(0, 0, part)
    arrived(1, 0)
    far(0, part, part)

    def one_block(block, carry):
        complete(block, 0)
        arrived(block, 1)
        near(block, 0, total)
        complete(block, 1)
        arrived(block + 1, 0)
        pl.when(block + 1 == WHOLE)(lambda: arrived(WHOLE, 1))
        far(block, 0, total)
        return carry

    lax.fori_loop(1, WHOLE, one_block, 0)
    rows = PART * TM // 2
    complete(WHOLE, 0)
    complete(WHOLE, 1)
    full(WHOLE, 0, rows)
    arrived(WHOLE + 1, 0)
    arrived(WHOLE + 1, 1)
    full(WHOLE, rows, rows)
    complete(WHOLE + 1, 0)
    complete(WHOLE + 1, 1)
    for block in range(blocks):
        wait_rows(send_sem.at[block], block, 1 + 2 * len(PEERS))


def second_steps(blocks, rows):
    left = [(WHOLE, step) for step in range(PART * TM // STEP, rows // STEP)]
    return left + [(block, step) for block in range(WHOLE + 1, blocks) for step in range(rows // STEP)]


def second_kernel(blocks, a, b, c, out, stage, out_sem, c_sem):
    order = second_steps(blocks, a.shape[0])

    def done_copy(block):
        rows = pl.ds(0, a.shape[0] if block < WHOLE else PART * TM)
        return pltpu.make_async_copy(
            c.at[block, rows, :], out.at[rows, pl.ds(block * W, W)], c_sem.at[block]
        )

    for block in range(WHOLE + 1):
        done_copy(block).start()

    def out_copy(slot):
        block, step = order[slot]
        return pltpu.make_async_copy(
            stage.at[slot], out.at[pl.ds(step * STEP, STEP), pl.ds(block * W, W)], out_sem.at[slot]
        )

    def flush(block, step, accs):
        slot = order.index((block, step))
        for unit in range(2):
            stage[slot, pl.ds(unit * HALF, HALF), :] = pltpu.matmul_pop(accs[unit]).astype(BF16)
        out_copy(slot).start()

    def body(*accs):
        steps = Steps(accs, a, b, flush)
        for at, (block, step) in enumerate(order):
            steps.step(block, step, range(6), (order[at + 1][0], 0) if at + 1 < len(order) else None)
        steps.drain()

    pl.run_scoped(body, *[pltpu.ACC(unit)((HALF, W), F32) for unit in (0, 0, 1, 1)])
    for slot in range(len(order)):
        out_copy(slot).wait()
    for block in range(WHOLE + 1):
        done_copy(block).wait()


def solution(mesh):
    def step(a, b):
        (rows, depth), columns = a.shape, b.shape[1]
        blocks, tiles = columns // W, rows // TM
        slots = len(second_steps(blocks, rows))
        dma = pltpu.SemaphoreType.DMA
        vmem, hbm = pl.BlockSpec(memory_space=pltpu.VMEM), pl.BlockSpec(memory_space=pltpu.HBM)
        a, b, c = pl.pallas_call(
            lambda *refs: first_kernel(blocks, *refs),
            name="first",
            out_shape=(
                pltpu.VMEM((rows, depth), BF16),
                pltpu.VMEM((blocks, depth, W), BF16),
                pltpu.VMEM((WHOLE + 1, rows, W), BF16),
            ),
            in_specs=[hbm, hbm],
            out_specs=(vmem, vmem, vmem),
            scratch_shapes=[
                pltpu.VMEM((rows, W), F32),
                dma((blocks,)),
                dma((tiles, 4)),
                dma((blocks,)),
                dma((blocks, 2)),
                dma((blocks, 2)),
                pltpu.SemaphoreType.REGULAR,
            ],
            compiler_params=pltpu.CompilerParams(
                vmem_limit_bytes=LIMIT, collective_id=0, has_side_effects=True
            ),
        )(a, b)
        a, b, c = (pltpu.with_memory_space_constraint(x, pltpu.VMEM) for x in (a, b, c))
        return pl.pallas_call(
            lambda *refs: second_kernel(blocks, *refs),
            name="second",
            out_shape=jax.ShapeDtypeStruct((rows, columns), BF16),
            in_specs=[vmem, vmem, vmem],
            out_specs=hbm,
            scratch_shapes=[pltpu.VMEM((slots, STEP, W), BF16), dma((slots,)), dma((WHOLE + 1,))],
            compiler_params=pltpu.CompilerParams(vmem_limit_bytes=LIMIT),
        )(a, b, c)

    spec = P("fsdp", None)
    return jax.shard_map(step, mesh=mesh, in_specs=(spec, spec), out_specs=spec, check_vma=False)
```

time: 44.4 us -> 43.4 us (0.977)
  Pallas kernels: 44.1 us -> 43.1 us
    pallas_call x1, Pallas kernels: 36.5 us -> 35.6 us  [step(): pl.pallas_call(lambda *refs: first_kernel(blocks, *refs), name='first', o...]
where the time goes in v3:
time: 43.4 us; the launch traced here: 43.3 us
  Pallas kernels  43.1 us (99%)
    pallas_call x1, Pallas kernels, step(): pl.pallas_call(lambda *refs: first_kernel(blocks, *refs), name='first', o...  35.6 us
    pallas_call x1, Pallas kernels, step(): pl.pallas_call(lambda *refs: second_kernel(blocks, *refs), name='second',...  7.57 us

profile of v3, /device:TPU:0, one launch (start us, length us, event | category | flops | bytes accessed | tf_op | source)
XLA Modules:
  0.0 43.3 jit_solution(5228681991085854340)
XLA Ops:
  0.0 35.6 %first.1 = (bf16[6144,1536]{1,0:T(8,128)(2,1)S(1)}, bf16[6,1536,256]{2,1,0:T(8,128)(2,1)S(1)}, bf16[5,6144,256]{2,1,0:T(8,128)(2,1)S(1)}) custom-call(bf16[6144,1536]{1,0:T(8,128)(2,1)} %refs_0_.1, bf16[96,1536]{1,0:T(8,128)(2,1)} %refs_1_.1), custom_call_target="tpu_custom_call" | custom-call | tf_op jit(solution)/shard_map/first/pallas_call | solution.py:269
  35.6 7.6 %second.1 = bf16[6144,1536]{1,0:T(8,128)(2,1)} custom-call(bf16[6144,1536]{1,0:T(8,128)(2,1)S(1)} %get-tuple-element.8.refs_0_, bf16[6,1536,256]{2,1,0:T(8,128)(2,1)S(1)} %get-tuple-element.9.refs_1_, bf16[5,6144,256]{2,1,0:T(8,128)(2,1)S(1)} %get-tuple-element.10.refs_2_), custom_call_target="tpu_custom_call" | custom-call | tf_op jit(solution)/shard_map/second/pallas_call | solution.py:293

commit v4 on v3

--- a/solution.py
+++ b/solution.py
@@ -176,7 +176,6 @@
         dots(first, count, each)
 
     total = a.shape[0]
-    part = total // 2
 
     arrived(0, 0)
     for tile in range(tiles):
@@ -189,9 +188,8 @@
     arrived(0, 1)
     near(0, early, total - early)
     complete(0, 1)
-    far(0, 0, part)
     arrived(1, 0)
-    far(0, part, part)
+    far(0, 0, total)
 
     def one_block(block, carry):
         complete(block, 0)

time: 43.4 us -> 43.4 us (level)
  no operation moved by 1% of the time
where the time goes in v4:
time: 43.4 us; the launch traced here: 43.3 us
  Pallas kernels  43.1 us (99%)
    pallas_call x1, Pallas kernels, step(): pl.pallas_call(lambda *refs: first_kernel(blocks, *refs), name='first', o...  35.6 us
    pallas_call x1, Pallas kernels, step(): pl.pallas_call(lambda *refs: second_kernel(blocks, *refs), name='second',...  7.57 us

profile of v4, /device:TPU:0, one launch (start us, length us, event | category | flops | bytes accessed | tf_op | source)
XLA Modules:
  0.0 43.3 jit_solution(6107180379559865449)
XLA Ops:
  0.0 35.6 %first.1 = (bf16[6144,1536]{1,0:T(8,128)(2,1)S(1)}, bf16[6,1536,256]{2,1,0:T(8,128)(2,1)S(1)}, bf16[5,6144,256]{2,1,0:T(8,128)(2,1)S(1)}) custom-call(bf16[6144,1536]{1,0:T(8,128)(2,1)} %refs_0_.1, bf16[96,1536]{1,0:T(8,128)(2,1)} %refs_1_.1), custom_call_target="tpu_custom_call" | custom-call | tf_op jit(solution)/shard_map/first/pallas_call | solution.py:267
  35.6 7.6 %second.1 = bf16[6144,1536]{1,0:T(8,128)(2,1)} custom-call(bf16[6144,1536]{1,0:T(8,128)(2,1)S(1)} %get-tuple-element.8.refs_0_, bf16[6,1536,256]{2,1,0:T(8,128)(2,1)S(1)} %get-tuple-element.9.refs_1_, bf16[5,6144,256]{2,1,0:T(8,128)(2,1)S(1)} %get-tuple-element.10.refs_2_), custom_call_target="tpu_custom_call" | custom-call | tf_op jit(solution)/shard_map/second/pallas_call | solution.py:291
